TPU v7x, 32 devices: a whole 2x2x4 slice. The times are simulated.
32 devices in a mesh: dp: 4 (over z), ctx: 8 (over y, x, core).
Axes of the slice: x: 2, y: 2, z: 4, core: 2. Of those that a mesh axis runs over, the one named last changes fastest.
Arguments:
- tokens: bfloat16 [4, 4096, 1024], P('dp', 'ctx'), may hold values from -60 to 60
- kept: int32 [4, 2048], P('dp', 'ctx'), may hold values from 0 to 4095, as said below
- gain_attn: float32 [1024], replicated, may hold values from 0.25 to 1.75
- gain_ffn: float32 [1024], replicated, may hold values from 0.25 to 1.75
- w_query: bfloat16 [1024, 512], P(None, 'ctx'), may hold values from -4 to 4
- w_key: bfloat16 [1024, 512], P(None, 'ctx'), may hold values from -4 to 4
- w_value: bfloat16 [1024, 512], P(None, 'ctx'), may hold values from -0.1875 to 0.1875
- w_out: bfloat16 [512, 1024], P('ctx'), may hold values from -0.25 to 0.25
- expert_ids: int32 [4, 2048, 1], P('dp', 'ctx'), may hold values from 0 to 31; in each aligned block of 256 rows (0 to 255, 256 to 511, ..., all dimensions but the last counted through in order) at most 16 rows name the same one
- w_in: bfloat16 [32, 1024, 2816], P(('dp', 'ctx')), may hold values from -0.1875 to 0.1875
- w_back: bfloat16 [32, 2816, 1024], P(('dp', 'ctx')), may hold values from -0.109375 to 0.109375
Outputs:
- blended: bfloat16 [4, 4096, 1024], P('dp', 'ctx')
Inputs may be any that keep to these rules, and one draw needn't show every extreme that they name: `kept`: in each document row, entries j * 256 to (j + 1) * 256 - 1 are strictly increasing positions from j * 512 to (j + 1) * 512 - 1. `expert_ids`: in each aligned block of 256 rows (the kept positions of one block b) no expert is named more than 16 times.
All inputs are finite; a program needn't handle non-finite values.
Results may differ from a plain program's by a relative error of at most 0.007.
Values may be sent and summed in bfloat16 or wider, within the bound.
A program may use at most 64 MiB of HBM per device.

v0:
```python
import functools
import math

import jax
import jax.numpy as jnp
from jax import lax
from jax.experimental import pallas as pl
from jax.experimental.pallas import tpu as pltpu
from jax.sharding import PartitionSpec as P

HS = 64
MESH = pl.DeviceIdType.MESH
LAST = (((1,), (1,)), ((), ()))

eps_norm = 1e-06
score_gain = 2.5


def rms_scale(values, gain):
    values = values.astype(jnp.float32)
    power = jnp.mean(values * values, axis=-1, keepdims=True)
    return values * lax.rsqrt(power + eps_norm) * gain


class Gather:
    def __init__(self, n, me, own, slots, send, recv):
        self.n, self.me, self.own, self.slots = n, me, own, slots
        self.send, self.recv = send, recv
        self.core, self.chip = me % 2, me // 2
        self.partner = me + 1 - 2 * self.core
        self.started = []

    def copy(self, ident, src, dst, target):
        return pltpu.make_async_remote_copy(
            src_ref=src,
            dst_ref=dst,
            send_sem=self.send.at[ident],
            recv_sem=self.recv.at[ident],
            device_id={"ctx": target},
            device_id_type=MESH,
        )

    def peers(self):
        chips = self.n // 2
        if chips == 4:
            x, y = self.chip % 2, self.chip // 2
            nx, ny = y * 2 + (1 - x), (1 - y) * 2 + x
            return [(nx, nx), (ny, ny)]
        return [
            ((self.chip + d) % chips, (self.chip + chips - d) % chips) for d in range(1, chips)
        ]

    def begin(self):
        own_to = self.slots.at[self.me]
        self.first = [
            self.copy(i, self.own, own_to, to * 2 + self.core)
            for i, (to, _) in enumerate(self.peers())
        ]
        self.base = len(self.first)
        self.twin = self.copy(self.base, self.own, own_to, self.partner)
        for c in self.first:
            c.start()
        self.twin.start()
        self.started = self.first + [self.twin]

    def relay(self):
        here, self.passed, self.late = [], [], []
        ident = self.base + 1
        peers = self.peers()
        square = self.n // 2 == 4
        half = self.own.shape[0] // 2
        for i, (_, source) in enumerate(peers):
            self.first[i].wait_recv()
            block = source * 2 + self.core
            here.append(block)
            if square:
                piece = self.slots.at[block, pl.ds(i * half, half)]
                c = self.copy(ident, piece, piece, peers[1 - i][0] * 2 + self.core)
                c.start()
                self.late.append(c)
                ident += 1
            c = self.copy(ident, self.slots.at[block], self.slots.at[block], self.partner)
            c.start()
            self.passed.append((source * 2 + 1 - self.core, c))
            ident += 1
        self.ident = ident
        self.started += self.late + [c for _, c in self.passed]
        return here

    def diagonal(self):
        if not self.late:
            return None
        block = (3 - self.chip) * 2 + self.core
        half = self.own.shape[0] // 2
        self.last = []
        for i, c in enumerate(self.late):
            c.wait_recv()
            piece = self.slots.at[block, pl.ds(i * half, half)]
            c = self.copy(self.ident + i, piece, piece, self.partner)
            c.start()
            self.last.append(c)
        self.started += self.last
        return block

    def final(self):
        if not self.late:
            return None
        for c in self.last:
            c.wait_recv()
        return (3 - self.chip) * 2 + 1 - self.core

    def drain(self):
        for c in self.started:
            c.wait_send()


def gather_copies(n):
    return 9 if n // 2 == 4 else 2 * (n // 2) - 1


def attention_kernel(
    n,
    heads,
    x_ref,
    wq_ref,
    wk_ref,
    wv_ref,
    wo_ref,
    mixed_ref,
    wo_all,
    x_all,
    q_all,
    k_all,
    v_all,
    stage,
    x_send,
    x_recv,
    o_send,
    o_recv,
    m_send,
    m_recv,
):
    me = lax.axis_index("ctx")
    rows = x_ref.shape[0]
    barrier = pltpu.get_barrier_semaphore()
    for d in range(1, n):
        pl.semaphore_signal(
            barrier, inc=1, device_id={"ctx": (me + d) % n}, device_id_type=MESH
        )
    pl.semaphore_wait(barrier, n - 1)

    def project(block, value):
        at = pl.ds(pl.multiple_of(block * rows, rows), rows)
        for h in range(heads):
            cols = pl.ds(h * HS, HS)
            q_all[h, at, :] = lax.dot_general(
                value, wq_ref[cols, :], LAST, preferred_element_type=jnp.float32
            ).astype(jnp.bfloat16)
            k_all[h, at, :] = lax.dot_general(
                value, wk_ref[cols, :], LAST, preferred_element_type=jnp.float32
            ).astype(jnp.bfloat16)
        v_all[:, at] = lax.dot_general(
            wv_ref[...], value, LAST, preferred_element_type=jnp.float32
        ).astype(jnp.bfloat16)

    g = Gather(n, me, x_ref, x_all, x_send, x_recv)
    o = Gather(n, me, wo_ref, wo_all, o_send, o_recv)
    g.begin()
    project(me, x_ref[...])
    wo_all[me] = wo_ref[...]
    g.twin.wait_recv()
    project(g.partner, x_all[g.partner])
    here = g.relay()
    o.begin()
    for block in here:
        project(block, x_all[block])
    for block, c in g.passed:
        c.wait_recv()
        project(block, x_all[block])
    block = g.diagonal()
    if block is not None:
        project(block, x_all[block])
    o.twin.wait_recv()
    o.relay()
    block = g.final()
    if block is not None:
        project(block, x_all[block])

    scale = score_gain / math.sqrt(HS) * math.log2(math.e)

    def send_block(step, target):
        return pltpu.make_async_remote_copy(
            src_ref=stage.at[step],
            dst_ref=mixed_ref.at[me],
            send_sem=m_send.at[step],
            recv_sem=m_recv.at[step],
            device_id={"ctx": target},
            device_id_type=MESH,
        )

    @pl.loop(0, n)
    def _(step):
        block = lax.rem(me + 1 + step, n)
        at = pl.ds(pl.multiple_of(block * rows, rows), rows)
        for h in range(heads):
            scores = lax.dot_general(
                k_all[h],
                q_all[h, at, :],
                LAST,
                preferred_element_type=jnp.float32,
            )
            top = jnp.max(scores, axis=0, keepdims=True)
            weights = jnp.exp2(scores * scale - top * scale)
            total = jnp.sum(weights, axis=0, keepdims=True)
            cols = pl.ds(h * HS, HS)
            mixed = jnp.dot(
                v_all[cols, :],
                weights.astype(jnp.bfloat16),
                preferred_element_type=jnp.float32,
            )
            stage[step, cols, :] = (mixed / total).astype(jnp.bfloat16)

        @pl.when(step < n - 1)
        def _():
            send_block(step, block).start()

    mixed_ref[me] = stage[n - 1]
    for _, c in o.passed:
        c.wait_recv()
    o.diagonal()
    o.final()

    @pl.loop(0, n - 1)
    def _(step):
        send_block(step, lax.rem(me + 1 + step, n)).wait()

    g.drain()
    o.drain()


def attention(normed, w_query, w_key, w_value, w_out):
    n = lax.axis_size("ctx")
    rows, width = normed.shape
    inner = w_query.shape[1]
    heads = inner // HS
    copies = gather_copies(n)
    vmem = pl.BlockSpec(memory_space=pltpu.VMEM)
    bf = jnp.bfloat16
    return pl.pallas_call(
        functools.partial(attention_kernel, n, heads),
        out_shape=(
            jax.ShapeDtypeStruct((n, inner, rows), bf),
            jax.ShapeDtypeStruct((n,) + w_out.shape, bf),
        ),
        in_specs=[vmem] * 5,
        out_specs=(vmem, vmem),
        scratch_shapes=[
            pltpu.VMEM((n, rows, width), bf),
            pltpu.VMEM((heads, n * rows, HS), bf),
            pltpu.VMEM((heads, n * rows, HS), bf),
            pltpu.VMEM((inner, n * rows), bf),
            pltpu.VMEM((n, inner, rows), bf),
            pltpu.SemaphoreType.DMA((copies,)),
            pltpu.SemaphoreType.DMA((copies,)),
            pltpu.SemaphoreType.DMA((copies,)),
            pltpu.SemaphoreType.DMA((copies,)),
            pltpu.SemaphoreType.DMA((n,)),
            pltpu.SemaphoreType.DMA((n,)),
        ],
        compiler_params=pltpu.CompilerParams(collective_id=0, has_side_effects=True),
        name="attention",
    )(normed, w_query.T, w_key.T, w_value.T, w_out)


def experts_plain(buffer, w_in, w_back, capacity):
    owners = lax.axis_size("dp") * lax.axis_size("ctx")
    expert_here, width = w_in.shape[0], buffer.shape[1]
    buffer = buffer.reshape(owners * expert_here, capacity, width)
    received = lax.all_to_all(buffer, ("dp", "ctx"), split_axis=0, concat_axis=0, tiled=True)
    grouped = received.reshape(owners, expert_here, capacity, width)
    hidden = jnp.einsum("sgid,gdf->sgif", grouped, w_in, preferred_element_type=jnp.float32)
    hidden = jnp.maximum(hidden, 0.0).astype(jnp.bfloat16)
    answer = jnp.einsum("sgif,gfd->sgid", hidden, w_back, preferred_element_type=jnp.float32)
    answered = answer.astype(jnp.bfloat16).reshape(owners * expert_here, capacity, width)
    back = lax.all_to_all(answered, ("dp", "ctx"), split_axis=0, concat_axis=0, tiled=True)
    return back.reshape(owners * expert_here * capacity, width)


def expert_kernel(
    planes,
    n,
    cap,
    buf_ref,
    w_in_hbm,
    w_back_hbm,
    back_ref,
    w_in_ref,
    w_back_ref,
    rows_ref,
    hidden_ref,
    answer_ref,
    w_sem,
    own_sem,
    d_send,
    d_recv,
    r_send,
    r_recv,
):
    dp, ctx = lax.axis_index("dp"), lax.axis_index("ctx")
    me = dp * n + ctx
    owners = planes * n
    loads = [
        pltpu.make_async_copy(w_in_hbm.at[0], w_in_ref, w_sem.at[0]),
        pltpu.make_async_copy(w_back_hbm.at[0], w_back_ref, w_sem.at[1]),
    ]
    for c in loads:
        c.start()
    barrier = pltpu.get_barrier_semaphore()

    @pl.loop(1, owners)
    def _(d):
        to = lax.rem(me + d, owners)
        pl.semaphore_signal(
            barrier, inc=1, device_id={"dp": to // n, "ctx": lax.rem(to, n)}, device_id_type=MESH
        )

    pl.semaphore_wait(barrier, owners - 1)

    def seat(index):
        return pl.ds(pl.multiple_of(index * cap, cap), cap)

    def at(shift):
        plane_shift, place_shift = shift // n, lax.rem(shift, n)
        half = planes // 2
        side = dp // half
        side = lax.rem(side + plane_shift // half, 2)
        plane = side * half + lax.rem(dp + plane_shift, half)
        return plane, lax.rem(ctx + place_shift, n)

    def dispatch(shift):
        plane, place = at(shift)
        return pltpu.make_async_remote_copy(
            src_ref=buf_ref.at[seat(plane * n + place)],
            dst_ref=rows_ref.at[seat(me)],
            send_sem=d_send.at[shift],
            recv_sem=d_recv.at[shift],
            device_id={"dp": plane, "ctx": place},
            device_id_type=MESH,
        )

    def give_back(shift):
        plane, place = at(shift)
        return pltpu.make_async_remote_copy(
            src_ref=answer_ref.at[seat(plane * n + place)],
            dst_ref=back_ref.at[seat(me)],
            send_sem=r_send.at[shift],
            recv_sem=r_recv.at[shift],
            device_id={"dp": plane, "ctx": place},
            device_id_type=MESH,
        )

    near = owners // 2

    @pl.loop(0, near)
    def _(shift):
        dispatch(near + shift).start()

        @pl.when(shift > 0)
        def _():
            dispatch(shift).start()

    own_in = pltpu.make_async_copy(buf_ref.at[seat(me)], rows_ref.at[seat(me)], own_sem.at[0])
    own_in.start()

    def run(first_row, count):
        inner = hidden_ref.shape[1]
        width = answer_ref.shape[1]
        take = pl.ds(pl.multiple_of(first_row, count), count)
        value = rows_ref[take, :]

        @pl.loop(0, inner // 256)
        def _(f):
            cols = pl.ds(pl.multiple_of(f * 256, 256), 256)
            hidden = jnp.dot(value, w_in_ref[:, cols], preferred_element_type=jnp.float32)
            hidden_ref[:, cols] = jnp.maximum(hidden, 0.0).astype(jnp.bfloat16)

        @pl.loop(0, width // 256)
        def _(f):
            cols = pl.ds(pl.multiple_of(f * 256, 256), 256)
            answer_ref[take, cols] = jnp.dot(
                hidden_ref[...], w_back_ref[:, cols], preferred_element_type=jnp.float32
            ).astype(jnp.bfloat16)

    half_rows = near * cap
    side = dp // (planes // 2)

    @pl.loop(1, near)
    def _(shift):
        dispatch(shift).wait_recv()

    own_in.wait()
    for c in loads:
        c.wait()

    @pl.loop(0, 2)
    def _(turn):
        @pl.when(turn == 1)
        def _():
            @pl.loop(near, owners)
            def _(shift):
                dispatch(shift).wait_recv()

        run(lax.rem(side + turn, 2) * half_rows, half_rows)

        @pl.loop(0, near)
        def _(shift):
            @pl.when(turn * near + shift > 0)
            def _():
                give_back(turn * near + shift).start()

    own_out = pltpu.make_async_copy(answer_ref.at[seat(me)], back_ref.at[seat(me)], own_sem.at[1])
    own_out.start()

    @pl.loop(1, owners)
    def _(shift):
        dispatch(shift).wait_send()
        give_back(shift).wait()

    own_out.wait()


def experts_fused(buffer, w_in, w_back, capacity):
    planes, n = lax.axis_size("dp"), lax.axis_size("ctx")
    owners = planes * n
    slots, width = buffer.shape
    inner = w_in.shape[2]
    bf = jnp.bfloat16
    vmem = pl.BlockSpec(memory_space=pltpu.VMEM)
    hbm = pl.BlockSpec(memory_space=pl.ANY)
    return pl.pallas_call(
        functools.partial(expert_kernel, planes, n, capacity),
        out_shape=jax.ShapeDtypeStruct((slots, width), bf),
        in_specs=[vmem, hbm, hbm],
        out_specs=vmem,
        scratch_shapes=[
            pltpu.VMEM(w_in.shape[1:], bf),
            pltpu.VMEM(w_back.shape[1:], bf),
            pltpu.VMEM((slots, width), bf),
            pltpu.VMEM((slots // 2, inner), bf),
            pltpu.VMEM((slots, width), bf),
            pltpu.SemaphoreType.DMA((2,)),
            pltpu.SemaphoreType.DMA((2,)),
            pltpu.SemaphoreType.DMA((owners,)),
            pltpu.SemaphoreType.DMA((owners,)),
            pltpu.SemaphoreType.DMA((owners,)),
            pltpu.SemaphoreType.DMA((owners,)),
        ],
        compiler_params=pltpu.CompilerParams(collective_id=1, has_side_effects=True),
        name="experts",
    )(buffer, w_in, w_back)


def experts(buffer, w_in, w_back, capacity):
    if capacity % 16 == 0 and w_in.shape[0] == 1:
        return experts_fused(buffer, w_in, w_back, capacity)
    return experts_plain(buffer, w_in, w_back, capacity)


def whole_kernel(
    planes,
    n,
    cap,
    kept_hbm,
    ids_hbm,
    gain_attn_hbm,
    gain_ffn_hbm,
    doc_hbm,
    wq_hbm,
    wk_hbm,
    wv_hbm,
    wo_hbm,
    w_in_hbm,
    w_back_hbm,
    out_ref,
    kept_ref,
    ids_ref,
    gain_attn_ref,
    gain_ffn_ref,
    doc_ref,
    w3_ref,
    wo_ref,
    w_in_ref,
    w_back_ref,
    place_all,
    x_all,
    q_all,
    k_all,
    v_all,
    mix_ref,
    m_out,
    m_in,
    wo_all,
    r_out,
    r_in,
    first_ref,
    ffn_ref,
    hidden_ref,
    second_ref,
    back_ref,
    picks_ref,
    acc_ref,
    w_sem,
    p_send,
    p_recv,
    x_send,
    x_recv,
    o_send,
    o_recv,
    r_send,
    r_recv,
    m_send,
    m_recv,
    b_send,
    b_recv,
    ready,
):
    f32, bf = jnp.float32, jnp.bfloat16
    dp, me = lax.axis_index("dp"), lax.axis_index("ctx")
    owners = planes * n
    rows, width = x_all.shape[1], x_all.shape[2]
    shard = doc_ref.shape[0]
    inner = hidden_ref.shape[1]
    wide = 2 * HS
    share = n * cap
    pairs = n // 2

    loads = [
        pltpu.make_async_copy(ids_hbm, ids_ref, w_sem.at[8]),
        pltpu.make_async_copy(kept_hbm, kept_ref, w_sem.at[9]),
        pltpu.make_async_copy(doc_hbm, doc_ref, w_sem.at[0]),
        pltpu.make_async_copy(gain_attn_hbm, gain_attn_ref, w_sem.at[10]),
        pltpu.make_async_copy(gain_ffn_hbm, gain_ffn_ref, w_sem.at[11]),
        pltpu.make_async_copy(wq_hbm, w3_ref.at[pl.ds(0, HS)], w_sem.at[1]),
        pltpu.make_async_copy(wk_hbm, w3_ref.at[pl.ds(2 * HS, HS)], w_sem.at[2]),
        pltpu.make_async_copy(wv_hbm, w3_ref.at[pl.ds(4 * HS, HS)], w_sem.at[3]),
        pltpu.make_async_copy(wv_hbm, w3_ref.at[pl.ds(7 * HS, HS)], w_sem.at[4]),
        pltpu.make_async_copy(wo_hbm, wo_ref, w_sem.at[5]),
        pltpu.make_async_copy(w_in_hbm.at[0], w_in_ref, w_sem.at[6]),
        pltpu.make_async_copy(w_back_hbm.at[0], w_back_ref, w_sem.at[7]),
    ]
    for c in loads:
        c.start()

    barrier = pltpu.get_barrier_semaphore()

    for d in range(1, n):
        pl.semaphore_signal(
            barrier, inc=1, device_id={"ctx": lax.rem(me + d, n)}, device_id_type=MESH
        )

    def column(sem):
        for d in range(1, planes):
            pl.semaphore_signal(
                sem, inc=1, device_id={"dp": lax.rem(dp + d, planes)}, device_id_type=MESH
            )

    column(barrier)

    def plane(g):
        high = lax.rem(dp // 2 + g // 2, 2)
        return high * 2 + lax.rem(dp + lax.rem(g, 2), 2)

    def one_hot(mask):
        return jnp.where(mask, 1.0, 0.0).astype(bf)

    def iota(shape, dim):
        return lax.broadcasted_iota(jnp.int32, shape, dim)

    blank = jnp.zeros((HS, width), bf)
    for i in (1, 3, 5, 6):
        w3_ref[pl.ds(i * HS, HS), :] = blank

    loads[0].wait()
    ids = ids_ref[...]
    named = one_hot(iota((owners, rows), 0) == ids)
    earlier = one_hot(iota((rows, rows), 0) < iota((rows, rows), 1))
    before = jnp.dot(named, earlier, preferred_element_type=f32)
    slot = jnp.sum(named.astype(f32) * before, axis=0, keepdims=True).astype(jnp.int32)
    place_own = ids * cap + slot
    place_all[me] = jnp.broadcast_to(place_own, place_all.shape[1:])

    loads[1].wait()
    local = kept_ref[...] - me * shard
    picks = one_hot(iota((shard, rows), 0) == local)
    for z in range(planes):
        cells = one_hot(iota((share, rows), 0) + z * share == place_own)
        picks_ref[z] = lax.dot_general(picks, cells, LAST, preferred_element_type=f32).astype(bf)
    loads[2].wait()
    x_all[me] = lax.dot_general(
        picks, doc_ref[...], (((0,), (0,)), ((), ())), preferred_element_type=f32
    ).astype(bf)

    for c in loads[3:10]:
        c.wait()
    pl.semaphore_wait(barrier, n + planes - 2)
    column(ready)

    def place_copy(d):
        return pltpu.make_async_remote_copy(
            src_ref=place_all.at[me],
            dst_ref=place_all.at[me],
            send_sem=p_send.at[d],
            recv_sem=p_recv.at[d],
            device_id={"ctx": lax.rem(me + d, n)},
            device_id_type=MESH,
        )

    for d in range(1, n):
        place_copy(d).start()

    o = Gather(n, me, wo_ref, wo_all, o_send, o_recv)
    core, chip, partner = o.core, o.chip, o.partner
    (near_x, _), (near_y, _) = o.peers()
    near_a = jnp.where(core == 0, near_x, near_y)
    near_b = jnp.where(core == 0, near_y, near_x)
    part = rows // 2

    def whole_block(ident, block, target):
        ref = x_all.at[block]
        return pltpu.make_async_remote_copy(
            src_ref=ref,
            dst_ref=ref,
            send_sem=x_send.at[ident],
            recv_sem=x_recv.at[ident],
            device_id={"ctx": target},
            device_id_type=MESH,
        )

    def half_block(ident, block, which, target):
        ref = x_all.at[block, pl.ds(pl.multiple_of(which * part, part), part)]
        return pltpu.make_async_remote_copy(
            src_ref=ref,
            dst_ref=ref,
            send_sem=x_send.at[ident],
            recv_sem=x_recv.at[ident],
            device_id={"ctx": target},
            device_id_type=MESH,
        )

    from_a, from_b, across = near_a * 2 + core, near_b * 2 + core, (3 - chip) * 2 + core
    own_a = whole_block(0, me, from_a)
    own_b = whole_block(1, me, from_b)
    twin = whole_block(2, me, partner)
    pass_a = whole_block(3, from_a, partner)
    pass_b = whole_block(4, from_b, partner)
    relay_a = half_block(5, from_a, core, from_b)
    relay_b = half_block(6, from_b, 1 - core, from_a)
    pass_c = half_block(7, across, core, partner)
    pass_d = half_block(8, across, 1 - core, partner)
    own_a.start()
    twin.start()

    def row_copy(turn, block):
        return pltpu.make_async_remote_copy(
            src_ref=r_out.at[turn - 1, block],
            dst_ref=r_in.at[dp, block],
            send_sem=r_send.at[turn * n + block],
            recv_sem=r_recv.at[turn * n + block],
            device_id={"dp": plane(turn)},
            device_id_type=MESH,
        )

    def route(block, value):
        index = iota((planes * cap, rows), 0)
        turn, s = index // cap, index % cap
        high = (dp // 2 + turn // 2) % 2
        to = high * 2 + (dp + turn % 2) % 2
        cell = (to * n + me) * cap + s
        taken = jnp.dot(
            one_hot(cell == place_all[block][0:1, :]), value, preferred_element_type=f32
        ).astype(bf)
        r_in[dp, block] = taken[0:cap]
        for turn in (2, 3, 1):
            r_out[turn - 1, block] = taken[turn * cap : (turn + 1) * cap]
            row_copy(turn, block).start()

    def project(block, value):
        at = pl.ds(pl.multiple_of(block * rows, rows), rows)
        normed = rms_scale(value, gain_attn_ref[...]).astype(bf)
        three = lax.dot_general(normed, w3_ref[...], LAST, preferred_element_type=f32)
        q_all[at, :] = three[:, 0:wide].astype(bf)
        k_all[at, :] = three[:, wide : 2 * wide].astype(bf)
        lane = iota((rows, wide), 1)
        v_all[0, at, :] = jnp.where(lane < HS, three[:, 2 * wide : 3 * wide], 1.0).astype(bf)
        v_all[1, at, :] = jnp.where(lane < HS, 1.0, three[:, 3 * wide : 4 * wide]).astype(bf)

    def take(block):
        value = x_all[block]
        route(block, value)
        project(block, value)

    take(me)
    wo_all[me] = wo_ref[...]
    for d in range(1, n):
        place_copy(d).wait_recv()
    twin.wait_recv()
    take(partner)
    own_a.wait_send()
    own_b.start()
    own_a.wait_recv()
    pass_a.start()
    relay_a.start()
    take(from_a)
    pass_a.wait_recv()
    take(near_b * 2 + 1 - core)
    own_b.wait_recv()
    pass_b.start()
    relay_b.start()
    take(from_b)
    pass_b.wait_recv()
    take(near_a * 2 + 1 - core)
    relay_a.wait_recv()
    pass_c.start()
    relay_b.wait_recv()
    pass_d.start()
    o.begin()
    take(across)
    pass_c.wait_recv()
    pass_d.wait_recv()
    take((3 - chip) * 2 + 1 - core)

    scale = score_gain / math.sqrt(HS) * math.log2(math.e)

    def mixed_copy(turn, d, j):
        to, c = plane(turn), lax.rem(me + d, n)
        lanes = pl.ds(pl.multiple_of(me * wide, wide), wide)
        return pltpu.make_async_remote_copy(
            src_ref=m_out.at[to * n + c, j],
            dst_ref=m_in.at[dp, j, :, lanes],
            send_sem=m_send.at[(turn * n + d) * pairs + j],
            recv_sem=m_recv.at[(turn * n + d) * pairs + j],
            device_id={"dp": to, "ctx": c},
            device_id_type=MESH,
        )

    def each(turn, act):
        @pl.loop(0, n)
        def _(d):
            @pl.when(turn + d > 0)
            def _():
                act(turn, d)

    def mixed_copies(turn, act):
        def some(turn, d):
            for j in range(pairs):
                act(mixed_copy(turn, d, j))

        each(turn, some)

    def attend(first, last):
        @pl.loop(first, last)
        def _(j):
            for side in (0, 1):
                block = 2 * j + side
                at = pl.ds(pl.multiple_of(block * rows, rows), rows)
                scores = lax.dot_general(
                    q_all[at, :], k_all[...], LAST, preferred_element_type=f32
                )
                top = jnp.max(scores, axis=1, keepdims=True)
                weights = jnp.exp2(scores * scale - top * scale)
                both = jnp.dot(weights.astype(bf), v_all[side], preferred_element_type=f32)
                total = pltpu.roll(both, HS, 1)
                mine = (iota((rows, wide), 1) // HS) == side
                mix_ref[pl.ds(side * rows, rows), :] = jnp.where(mine, both / total, 0.0).astype(bf)
            places = jnp.concatenate([place_all[2 * j][0:1, :], place_all[2 * j + 1][0:1, :]], axis=1)
            spots = one_hot(iota((owners * cap, 2 * rows), 0) == places)
            spread = jnp.dot(spots, mix_ref[...], preferred_element_type=f32).astype(bf)
            m_out[:, j] = spread.reshape(owners, cap, wide)
            each(2, lambda turn, d: mixed_copy(turn, d, j).start())
            each(0, lambda turn, d: mixed_copy(turn, d, j).start())

    pl.semaphore_wait(ready, planes - 1)
    attend(0, pairs - 1)
    o.twin.wait_recv()
    o.relay()
    attend(pairs - 1, pairs)
    o.diagonal()

    def seat(t):
        return lax.rem(t, 2) * 2 + t // 2

    def back_copy(turn, d):
        to, c = plane(turn), lax.rem(me + d, n)
        return pltpu.make_async_remote_copy(
            src_ref=second_ref.at[to, lax.rem(c, 2), c // 2],
            dst_ref=back_ref.at[dp, me],
            send_sem=b_send.at[turn * n + d],
            recv_sem=b_recv.at[turn * n + d],
            device_id={"dp": to, "ctx": c},
            device_id_type=MESH,
        )

    mixed_copies(1, lambda c: c.start())
    mixed_copies(3, lambda c: c.start())
    m_in[dp, :, :, pl.ds(pl.multiple_of(me * wide, wide), wide)] = m_out[dp * n + me]
    for _, c in o.passed:
        c.wait_recv()
    o.final()
    touched = jnp.zeros((shard, 1), f32)
    for z in range(planes):
        touched = touched + jnp.sum(picks_ref[z].astype(f32), axis=1, keepdims=True)
    acc_ref[...] = jnp.where(touched > 0.5, 0.0, doc_ref[...].astype(f32))
    for c in loads[10:]:
        c.wait()

    half = pairs * cap

    @pl.loop(0, planes)
    def _(t):
        turn = seat(t)
        source = plane(turn)
        mixed_copies(turn, lambda c: c.wait_recv())

        @pl.when(turn > 0)
        def _():
            @pl.loop(0, n)
            def _(block):
                row_copy(turn, block).wait_recv()

        mixed = m_in[source].reshape(half, n * wide)
        heads = [mixed[:, h * wide : (h + 1) * wide] for h in range(n)]
        low = jnp.concatenate([h[:, :HS] for h in heads], axis=1)
        high = jnp.concatenate([h[:, HS:] for h in heads], axis=1)
        base = [r_in[source, 2 * j + side] for side in (0, 1) for j in range(pairs)]
        first_ref[...] = jnp.concatenate(base, axis=0).astype(f32) + jnp.dot(
            jnp.concatenate([low, high], axis=0),
            wo_all[...].reshape(n * HS, width),
            preferred_element_type=f32,
        )
        ffn_ref[...] = rms_scale(first_ref[...], gain_ffn_ref[...]).astype(bf)
        for f in range(0, inner, 256):
            hidden = jnp.dot(ffn_ref[...], w_in_ref[:, f : f + 256], preferred_element_type=f32)
            hidden_ref[:, f : f + 256] = jnp.maximum(hidden, 0.0).astype(bf)
        for f in range(0, width, 256):
            answer = jnp.dot(
                hidden_ref[...], w_back_ref[:, f : f + 256], preferred_element_type=f32
            ).astype(bf)
            second = (first_ref[:, f : f + 256] + answer.astype(f32)).astype(bf)
            second_ref[source, :, :, :, f : f + 256] = second.reshape(2, pairs, cap, 256)
        each(turn, lambda turn, d: back_copy(turn, d).start())

    back_ref[dp, me] = second_ref[dp, lax.rem(me, 2), me // 2]

    @pl.loop(0, planes)
    def _(t):
        turn = seat(t)
        source = plane(turn)
        each(turn, lambda turn, d: back_copy(turn, d).wait_recv())
        acc_ref[...] += jnp.dot(
            picks_ref[source], back_ref[source].reshape(share, width), preferred_element_type=f32
        )

    out_ref[...] = acc_ref[...].astype(bf)

    for d in range(1, n):
        place_copy(d).wait_send()

    @pl.loop(0, planes)
    def _(turn):
        mixed_copies(turn, lambda c: c.wait_send())
        each(turn, lambda turn, d: back_copy(turn, d).wait_send())

        @pl.when(turn > 0)
        def _():
            @pl.loop(0, n)
            def _(block):
                row_copy(turn, block).wait_send()

    for c in (own_b, twin, pass_a, pass_b, relay_a, relay_b, pass_c, pass_d):
        c.wait_send()
    o.drain()


def whole(document, kept, ids, gain_attn, gain_ffn, w_query, w_key, w_value, w_out, w_in, w_back):
    planes, n = lax.axis_size("dp"), lax.axis_size("ctx")
    owners = planes * n
    shard, width = document.shape
    rows = kept.shape[1]
    cap = 2 * rows // owners
    inner = w_in.shape[2]
    pairs = n // 2
    wide = 2 * HS
    half = pairs * cap
    bf, f32 = jnp.bfloat16, jnp.float32
    vmem = pl.BlockSpec(memory_space=pltpu.VMEM)
    hbm = pl.BlockSpec(memory_space=pltpu.HBM)
    sems = pltpu.SemaphoreType.DMA
    copies = gather_copies(n)
    grant = 42 * 1024 * 1024
    operands = (
        kept,
        ids,
        gain_attn.reshape(1, width),
        gain_ffn.reshape(1, width),
        document,
        w_query.T,
        w_key.T,
        w_value.T,
        w_out,
        w_in,
        w_back,
    )
    return pl.pallas_call(
        functools.partial(whole_kernel, planes, n, cap),
        out_shape=jax.ShapeDtypeStruct((shard, width), bf),
        in_specs=[hbm] * 11,
        out_specs=vmem,
        scratch_shapes=[
            pltpu.VMEM((1, rows), jnp.int32),
            pltpu.VMEM((1, rows), jnp.int32),
            pltpu.VMEM((1, width), f32),
            pltpu.VMEM((1, width), f32),
            pltpu.VMEM((shard, width), bf),
            pltpu.VMEM((8 * HS, width), bf),
            pltpu.VMEM(w_out.shape, bf),
            pltpu.VMEM(w_in.shape[1:], bf),
            pltpu.VMEM(w_back.shape[1:], bf),
            pltpu.VMEM((n, 8, rows), jnp.int32),
            pltpu.VMEM((n, rows, width), bf),
            pltpu.VMEM((n * rows, wide), bf),
            pltpu.VMEM((n * rows, wide), bf),
            pltpu.VMEM((2, n * rows, wide), bf),
            pltpu.VMEM((2 * rows, wide), bf),
            pltpu.VMEM((owners, pairs, cap, wide), bf),
            pltpu.VMEM((planes, pairs, cap, n * wide), bf),
            pltpu.VMEM((n,) + w_out.shape, bf),
            pltpu.VMEM((planes - 1, n, cap, width), bf),
            pltpu.VMEM((planes, n, cap, width), bf),
            pltpu.VMEM((2 * half, width), f32),
            pltpu.VMEM((2 * half, width), bf),
            pltpu.VMEM((2 * half, inner), bf),
            pltpu.VMEM((planes, 2, pairs, cap, width), bf),
            pltpu.VMEM((planes, n, cap, width), bf),
            pltpu.VMEM((planes, shard, n * cap), bf),
            pltpu.VMEM((shard, width), f32),
            sems((12,)),
            sems((n,)),
            sems((n,)),
            sems((copies,)),
            sems((copies,)),
            sems((copies,)),
            sems((copies,)),
            sems((owners,)),
            sems((owners,)),
            sems((owners * pairs,)),
            sems((owners * pairs,)),
            sems((owners,)),
            sems((owners,)),
            pltpu.SemaphoreType.REGULAR,
        ],
        compiler_params=pltpu.CompilerParams(
            collective_id=2, has_side_effects=True, vmem_limit_bytes=grant
        ),
        name="whole",
    )(*[pltpu.with_memory_space_constraint(a, pltpu.HBM) for a in operands])


def fits_whole(planes, n, keep_here, w_query, w_out, w_in):
    cap = 2 * keep_here // (planes * n)
    return (
        planes == 4
        and n == 8
        and w_query.shape[1] == HS
        and w_out.shape[0] == HS
        and w_in.shape[0] == 1
        and cap % 16 == 0
        and w_in.shape[2] % 256 == 0
    )


def body(
    tokens, kept, gain_attn, gain_ffn, w_query, w_key, w_value, w_out, expert_ids, w_in, w_back
):
    document = tokens[0]
    shard_len, width_model = document.shape
    ctx_count = lax.axis_size("ctx")
    dp_count = lax.axis_size("dp")
    if fits_whole(dp_count, ctx_count, kept.shape[1], w_query, w_out, w_in):
        ids = expert_ids.reshape(1, kept.shape[1])
        weights = (w_query, w_key, w_value, w_out, w_in, w_back)
        return whole(document, kept, ids, gain_attn, gain_ffn, *weights)[None]
    local = kept[0] - lax.axis_index("ctx") * shard_len
    keep_here = local.shape[0]
    positions = jnp.arange(shard_len, dtype=jnp.int32)
    picks = (local[:, None] == positions[None, :]).astype(jnp.bfloat16)
    rows = jnp.dot(picks, document, preferred_element_type=jnp.float32).astype(jnp.bfloat16)
    normed = rms_scale(rows, gain_attn).astype(jnp.bfloat16)
    mixed, w_out_all = attention(normed, w_query, w_key, w_value, w_out)
    inner_all = w_out.shape[0] * ctx_count
    attn = lax.dot_general(
        mixed.reshape(inner_all, keep_here),
        w_out_all.reshape(inner_all, width_model),
        (((0,), (0,)), ((), ())),
        preferred_element_type=jnp.float32,
    )
    first = rows.astype(jnp.float32) + attn
    ffn_in = rms_scale(first, gain_ffn).astype(jnp.bfloat16)
    expert_here = w_in.shape[0]
    owners = dp_count * ctx_count
    experts_all = expert_here * owners
    capacity = 2 * keep_here // experts_all
    labels = expert_ids[0, :, 0]
    order = jnp.arange(keep_here, dtype=jnp.int32)
    same = (labels[:, None] == labels[None, :]) & (order[None, :] < order[:, None])
    slots = jnp.sum(same.astype(jnp.int32), axis=1)
    place = labels * capacity + slots
    cells = jnp.arange(experts_all * capacity, dtype=jnp.int32)
    spots = (place[None, :] == cells[:, None]).astype(jnp.bfloat16)
    buffer = jnp.dot(spots, ffn_in, preferred_element_type=jnp.float32).astype(jnp.bfloat16)
    answers = experts(buffer, w_in, w_back, capacity)
    seats = (place[:, None] == cells[None, :]).astype(jnp.bfloat16)
    taken = jnp.dot(seats, answers, preferred_element_type=jnp.float32)
    second = (first + taken).astype(jnp.bfloat16)
    hits = positions[:, None] == local[None, :]
    fresh = jnp.dot(hits.astype(jnp.bfloat16), second, preferred_element_type=jnp.float32)
    touched = jnp.any(hits, axis=1, keepdims=True)
    blended = jnp.where(touched, fresh.astype(jnp.bfloat16), document)
    return blended[None]


def solution(mesh):
    return jax.shard_map(
        body,
        mesh=mesh,
        in_specs=(
            P("dp", "ctx", None),
            P("dp", "ctx"),
            P(),
            P(),
            P(None, "ctx"),
            P(None, "ctx"),
            P(None, "ctx"),
            P("ctx", None),
            P("dp", "ctx", None),
            P(("dp", "ctx"), None, None),
            P(("dp", "ctx"), None, None),
        ),
        out_specs=P("dp", "ctx", None),
        check_vma=False,
    )
```

profile of v0, /device:TPU:9, one launch (start us, length us, event | category | flops | bytes accessed | tf_op | source)
XLA Modules:
  0.0 75.1 jit_solution(7643657681925563738)
XLA Ops:
  0.0 74.1 %whole.1 = bf16[512,1024]{1,0:T(8,128)(2,1)S(1)} custom-call(s32[1,256]{1,0:T(1,128)} %kept_hbm.1, s32[1,256]{1,0:T(1,128)} %bitcast.15, f32[1,1024]{1,0:T(1,128)} %bitcast.13, f32[1,1024]{1,0:T(1,128)} %bitcast.14, bf16[512,1024]{1,0:T(8,128)(2,1)} %bitcast.9, bf16[64,1024]{1,0:T(8,128)(2,1)} %bitcast.10, bf16[64,1024]{1,0:T(8,128)(2,1)} %bitcast.11, ...), custom_call_target="tpu_custom_call" | custom-call | tf_op jit(solution)/shard_map/whole/pallas_call | solution.py:913
  74.1 1.0 %copy.13 = bf16[1,512,1024]{2,1,0:T(8,128)(2,1)} copy(bf16[1,512,1024]{2,1,0:T(8,128)(2,1)S(1)} %bitcast.8) | data formatting | bytes 2097152
where the time goes:
time: 75.3 us; the launch traced here: 75.1 us
  Pallas kernels  74.1 us (98%)
  local copies, waits for them, and re-layouts  0.97 us (1%)
    pallas_call x1, Pallas kernels, whole(): pl.pallas_call(functools.partial(whole_kernel, planes, n, cap), out_shape...  74.1 us

commit v1 on v0

--- a/solution.py
+++ b/solution.py
@@ -576,10 +576,6 @@
     def iota(shape, dim):
         return lax.broadcasted_iota(jnp.int32, shape, dim)
 
-    blank = jnp.zeros((HS, width), bf)
-    for i in (1, 3, 5, 6):
-        w3_ref[pl.ds(i * HS, HS), :] = blank
-
     loads[0].wait()
     ids = ids_ref[...]
     named = one_hot(iota((owners, rows), 0) == ids)
@@ -588,29 +584,35 @@
     slot = jnp.sum(named.astype(f32) * before, axis=0, keepdims=True).astype(jnp.int32)
     place_own = ids * cap + slot
     place_all[me] = jnp.broadcast_to(place_own, place_all.shape[1:])
-
     loads[1].wait()
     local = kept_ref[...] - me * shard
     picks = one_hot(iota((shard, rows), 0) == local)
-    for z in range(planes):
-        cells = one_hot(iota((share, rows), 0) + z * share == place_own)
-        picks_ref[z] = lax.dot_general(picks, cells, LAST, preferred_element_type=f32).astype(bf)
     loads[2].wait()
     x_all[me] = lax.dot_general(
         picks, doc_ref[...], (((0,), (0,)), ((), ())), preferred_element_type=f32
     ).astype(bf)
 
-    for c in loads[3:10]:
-        c.wait()
     pl.semaphore_wait(barrier, n + planes - 2)
     column(ready)
+
+    o = Gather(n, me, wo_ref, wo_all, o_send, o_recv)
+
+    def bulk(ref, sends, recvs):
+        return pltpu.make_async_remote_copy(
+            src_ref=ref,
+            dst_ref=ref,
+            send_sem=sends,
+            recv_sem=recvs,
+            device_id={"ctx": o.partner},
+            device_id_type=MESH,
+        )
 
     def place_copy(d):
         return pltpu.make_async_remote_copy(
             src_ref=place_all.at[me],
             dst_ref=place_all.at[me],
-            send_sem=p_send.at[d],
-            recv_sem=p_recv.at[d],
+            send_sem=p_send,
+            recv_sem=p_recv,
             device_id={"ctx": lax.rem(me + d, n)},
             device_id_type=MESH,
         )
@@ -618,15 +620,12 @@
     for d in range(1, n):
         place_copy(d).start()
 
-    o = Gather(n, me, wo_ref, wo_all, o_send, o_recv)
     core, chip, partner = o.core, o.chip, o.partner
     (near_x, _), (near_y, _) = o.peers()
-    near_a = jnp.where(core == 0, near_x, near_y)
-    near_b = jnp.where(core == 0, near_y, near_x)
-    part = rows // 2
-
-    def whole_block(ident, block, target):
-        ref = x_all.at[block]
+    part, piece = rows // 2, rows // 4
+
+    def send(ident, block, first, count, target):
+        ref = x_all.at[block, pl.ds(pl.multiple_of(first, count), count)]
         return pltpu.make_async_remote_copy(
             src_ref=ref,
             dst_ref=ref,
@@ -636,36 +635,47 @@
             device_id_type=MESH,
         )
 
-    def half_block(ident, block, which, target):
-        ref = x_all.at[block, pl.ds(pl.multiple_of(which * part, part), part)]
-        return pltpu.make_async_remote_copy(
-            src_ref=ref,
-            dst_ref=ref,
-            send_sem=x_send.at[ident],
-            recv_sem=x_recv.at[ident],
-            device_id={"ctx": target},
-            device_id_type=MESH,
-        )
-
-    from_a, from_b, across = near_a * 2 + core, near_b * 2 + core, (3 - chip) * 2 + core
-    own_a = whole_block(0, me, from_a)
-    own_b = whole_block(1, me, from_b)
-    twin = whole_block(2, me, partner)
-    pass_a = whole_block(3, from_a, partner)
-    pass_b = whole_block(4, from_b, partner)
-    relay_a = half_block(5, from_a, core, from_b)
-    relay_b = half_block(6, from_b, 1 - core, from_a)
-    pass_c = half_block(7, across, core, partner)
-    pass_d = half_block(8, across, 1 - core, partner)
-    own_a.start()
+    to_x, to_y = near_x * 2 + core, near_y * 2 + core
+    mine = core * part
+    twin = send(0, me, 0, rows, partner)
+    own, passed, relays, last = [], [], [], []
+    for k in (0, 1):
+        from_x, from_y, across = near_x * 2 + k, near_y * 2 + k, (3 - chip) * 2 + k
+        own.append(
+            (
+                send(1 + k, chip * 2 + k, mine, part, to_x),
+                send(3 + k, chip * 2 + k, mine, part, to_y),
+            )
+        )
+        passed.append(
+            (send(5 + k, from_x, mine, part, partner), send(7 + k, from_y, mine, part, partner))
+        )
+        relays.append(
+            (
+                send(9 + k, from_x, mine, piece, to_y),
+                send(11 + k, from_y, mine + piece, piece, to_x),
+            )
+        )
+        last.append(send(13 + k, across, mine, part, partner))
     twin.start()
+
+    @pl.when(core == 0)
+    def _():
+        for c in own[0]:
+            c.start()
+
+    blank = jnp.zeros((HS, width), bf)
+    for i in (1, 3, 5, 6):
+        w3_ref[pl.ds(i * HS, HS), :] = blank
+    for c in loads[3:10]:
+        c.wait()
 
     def row_copy(turn, block):
         return pltpu.make_async_remote_copy(
             src_ref=r_out.at[turn - 1, block],
             dst_ref=r_in.at[dp, block],
-            send_sem=r_send.at[turn * n + block],
-            recv_sem=r_recv.at[turn * n + block],
+            send_sem=r_send.at[turn],
+            recv_sem=r_recv.at[turn],
             device_id={"dp": plane(turn)},
             device_id_type=MESH,
         )
@@ -700,34 +710,39 @@
         project(block, value)
 
     take(me)
+    twin.wait_recv()
+
+    @pl.when(core == 1)
+    def _():
+        for c in own[0]:
+            c.start()
+
+    for c in own[1]:
+        c.start()
+    for z in range(planes):
+        cells = one_hot(iota((share, rows), 0) + z * share == place_own)
+        picks_ref[z] = lax.dot_general(picks, cells, LAST, preferred_element_type=f32).astype(bf)
     wo_all[me] = wo_ref[...]
-    for d in range(1, n):
-        place_copy(d).wait_recv()
-    twin.wait_recv()
+    places = bulk(place_all.at[pl.ds(0, n - 1)], p_send, p_recv)
+    places.wait_recv()
     take(partner)
-    own_a.wait_send()
-    own_b.start()
-    own_a.wait_recv()
-    pass_a.start()
-    relay_a.start()
-    take(from_a)
-    pass_a.wait_recv()
-    take(near_b * 2 + 1 - core)
-    own_b.wait_recv()
-    pass_b.start()
-    relay_b.start()
-    take(from_b)
-    pass_b.wait_recv()
-    take(near_a * 2 + 1 - core)
-    relay_a.wait_recv()
-    pass_c.start()
-    relay_b.wait_recv()
-    pass_d.start()
-    o.begin()
-    take(across)
-    pass_c.wait_recv()
-    pass_d.wait_recv()
-    take((3 - chip) * 2 + 1 - core)
+    for k in (0, 1):
+        for c, p, r in zip(own[k], passed[k], relays[k]):
+            c.wait_recv()
+            p.start()
+            r.start()
+        if k == 1:
+            o.begin()
+        for p, near in zip(passed[k], (near_x, near_y)):
+            p.wait_recv()
+            take(near * 2 + k)
+    for k in (0, 1):
+        for r in relays[k]:
+            r.wait_recv()
+        last[k].start()
+    for k in (0, 1):
+        last[k].wait_recv()
+        take((3 - chip) * 2 + k)
 
     scale = score_gain / math.sqrt(HS) * math.log2(math.e)
 
@@ -737,10 +752,16 @@
         return pltpu.make_async_remote_copy(
             src_ref=m_out.at[to * n + c, j],
             dst_ref=m_in.at[dp, j, :, lanes],
-            send_sem=m_send.at[(turn * n + d) * pairs + j],
-            recv_sem=m_recv.at[(turn * n + d) * pairs + j],
+            send_sem=m_send.at[turn],
+            recv_sem=m_recv.at[turn],
             device_id={"dp": to, "ctx": c},
             device_id_type=MESH,
+        )
+
+    def mixed_own(j):
+        lanes = pl.ds(pl.multiple_of(me * wide, wide), wide)
+        return pltpu.make_async_copy(
+            m_out.at[dp * n + me, j], m_in.at[dp, j, :, lanes], m_recv.at[0]
         )
 
     def each(turn, act):
@@ -778,6 +799,7 @@
             m_out[:, j] = spread.reshape(owners, cap, wide)
             each(2, lambda turn, d: mixed_copy(turn, d, j).start())
             each(0, lambda turn, d: mixed_copy(turn, d, j).start())
+            mixed_own(j).start()
 
     pl.semaphore_wait(ready, planes - 1)
     attend(0, pairs - 1)
@@ -787,31 +809,30 @@
     o.diagonal()
 
     def seat(t):
-        return lax.rem(t, 2) * 2 + t // 2
+        return lax.rem(t + planes // 2, planes)
 
     def back_copy(turn, d):
         to, c = plane(turn), lax.rem(me + d, n)
         return pltpu.make_async_remote_copy(
             src_ref=second_ref.at[to, lax.rem(c, 2), c // 2],
             dst_ref=back_ref.at[dp, me],
-            send_sem=b_send.at[turn * n + d],
-            recv_sem=b_recv.at[turn * n + d],
+            send_sem=b_send.at[turn],
+            recv_sem=b_recv.at[turn],
             device_id={"dp": to, "ctx": c},
             device_id_type=MESH,
         )
 
+    mixed_copies(3, lambda c: c.start())
     mixed_copies(1, lambda c: c.start())
-    mixed_copies(3, lambda c: c.start())
-    m_in[dp, :, :, pl.ds(pl.multiple_of(me * wide, wide), wide)] = m_out[dp * n + me]
-    for _, c in o.passed:
-        c.wait_recv()
-    o.final()
     touched = jnp.zeros((shard, 1), f32)
     for z in range(planes):
         touched = touched + jnp.sum(picks_ref[z].astype(f32), axis=1, keepdims=True)
     acc_ref[...] = jnp.where(touched > 0.5, 0.0, doc_ref[...].astype(f32))
     for c in loads[10:]:
         c.wait()
+    for _, c in o.passed:
+        c.wait_recv()
+    o.final()
 
     half = pairs * cap
 
@@ -819,13 +840,11 @@
     def _(t):
         turn = seat(t)
         source = plane(turn)
-        mixed_copies(turn, lambda c: c.wait_recv())
+        bulk(m_in.at[source], m_send.at[turn], m_recv.at[turn]).wait_recv()
 
         @pl.when(turn > 0)
         def _():
-            @pl.loop(0, n)
-            def _(block):
-                row_copy(turn, block).wait_recv()
+            bulk(r_in.at[source], r_send.at[turn], r_recv.at[turn]).wait_recv()
 
         mixed = m_in[source].reshape(half, n * wide)
         heads = [mixed[:, h * wide : (h + 1) * wide] for h in range(n)]
@@ -849,35 +868,35 @@
             second_ref[source, :, :, :, f : f + 256] = second.reshape(2, pairs, cap, 256)
         each(turn, lambda turn, d: back_copy(turn, d).start())
 
-    back_ref[dp, me] = second_ref[dp, lax.rem(me, 2), me // 2]
-
-    @pl.loop(0, planes)
-    def _(t):
-        turn = seat(t)
+    pltpu.make_async_copy(
+        second_ref.at[dp, lax.rem(me, 2), me // 2], back_ref.at[dp, me], b_recv.at[0]
+    ).start()
+
+    def returned(turn):
         source = plane(turn)
-        each(turn, lambda turn, d: back_copy(turn, d).wait_recv())
-        acc_ref[...] += jnp.dot(
+        bulk(back_ref.at[source], b_send.at[turn], b_recv.at[turn]).wait_recv()
+        return acc_ref[...] + jnp.dot(
             picks_ref[source], back_ref[source].reshape(share, width), preferred_element_type=f32
         )
 
-    out_ref[...] = acc_ref[...].astype(bf)
-
-    for d in range(1, n):
-        place_copy(d).wait_send()
-
-    @pl.loop(0, planes)
-    def _(turn):
-        mixed_copies(turn, lambda c: c.wait_send())
-        each(turn, lambda turn, d: back_copy(turn, d).wait_send())
-
-        @pl.when(turn > 0)
-        def _():
-            @pl.loop(0, n)
-            def _(block):
-                row_copy(turn, block).wait_send()
-
-    for c in (own_b, twin, pass_a, pass_b, relay_a, relay_b, pass_c, pass_d):
+    for turn in (0, 1, 2):
+        acc_ref[...] = returned(turn)
+
+    out_ref[...] = returned(3).astype(bf)
+
+    places.wait_send()
+
+    for turn in range(planes):
+        count = n - (turn == 0)
+        bulk(m_out.at[pl.ds(0, count)], m_send.at[turn], m_recv.at[turn]).wait_send()
+        bulk(back_ref.at[0, pl.ds(0, count)], b_send.at[turn], b_recv.at[turn]).wait_send()
+        if turn:
+            bulk(r_in.at[0], r_send.at[turn], r_recv.at[turn]).wait_send()
+    for c in (twin, *last):
         c.wait_send()
+    for c in own + passed + relays:
+        c[0].wait_send()
+        c[1].wait_send()
     o.drain()
 
 
@@ -944,18 +963,18 @@
             pltpu.VMEM((planes, shard, n * cap), bf),
             pltpu.VMEM((shard, width), f32),
             sems((12,)),
-            sems((n,)),
-            sems((n,)),
+            sems(()),
+            sems(()),
+            sems((15,)),
+            sems((15,)),
             sems((copies,)),
             sems((copies,)),
-            sems((copies,)),
-            sems((copies,)),
-            sems((owners,)),
-            sems((owners,)),
-            sems((owners * pairs,)),
-            sems((owners * pairs,)),
-            sems((owners,)),
-            sems((owners,)),
+            sems((planes,)),
+            sems((planes,)),
+            sems((planes,)),
+            sems((planes,)),
+            sems((planes,)),
+            sems((planes,)),
             pltpu.SemaphoreType.REGULAR,
         ],
         compiler_params=pltpu.CompilerParams(

time: 75.3 us -> 72.3 us (0.960)
  the two profiles are of different devices: /device:TPU:9 before, /device:TPU:0 now
where the time goes in v1:
time: 72.3 us; the launch traced here: 72.1 us
  Pallas kernels  71.2 us (98%)
  local copies, waits for them, and re-layouts  0.97 us (1%)
    pallas_call x1, Pallas kernels, whole(): pl.pallas_call(functools.partial(whole_kernel, planes, n, cap), out_shape...  71.2 us

profile of v1, /device:TPU:0, one launch (start us, length us, event | category | flops | bytes accessed | tf_op | source)
XLA Modules:
  0.0 72.1 jit_solution(13256555349888021001)
XLA Ops:
  0.0 71.2 %whole.1 = bf16[512,1024]{1,0:T(8,128)(2,1)S(1)} custom-call(s32[1,256]{1,0:T(1,128)} %kept_hbm.1, s32[1,256]{1,0:T(1,128)} %bitcast.15, f32[1,1024]{1,0:T(1,128)} %bitcast.13, f32[1,1024]{1,0:T(1,128)} %bitcast.14, bf16[512,1024]{1,0:T(8,128)(2,1)} %bitcast.9, bf16[64,1024]{1,0:T(8,128)(2,1)} %bitcast.10, bf16[64,1024]{1,0:T(8,128)(2,1)} %bitcast.11, ...), custom_call_target="tpu_custom_call" | custom-call | tf_op jit(solution)/shard_map/whole/pallas_call | solution.py:932
  71.2 1.0 %copy.13 = bf16[1,512,1024]{2,1,0:T(8,128)(2,1)} copy(bf16[1,512,1024]{2,1,0:T(8,128)(2,1)S(1)} %bitcast.8) | data formatting | bytes 2097152

commit v2 on v1

--- a/solution.py
+++ b/solution.py
@@ -496,7 +496,10 @@
     q_all,
     k_all,
     v_all,
+    sum_ref,
+    top_ref,
     mix_ref,
+    cells_ref,
     m_out,
     m_in,
     wo_all,
@@ -543,7 +546,6 @@
         pltpu.make_async_copy(wq_hbm, w3_ref.at[pl.ds(0, HS)], w_sem.at[1]),
         pltpu.make_async_copy(wk_hbm, w3_ref.at[pl.ds(2 * HS, HS)], w_sem.at[2]),
         pltpu.make_async_copy(wv_hbm, w3_ref.at[pl.ds(4 * HS, HS)], w_sem.at[3]),
-        pltpu.make_async_copy(wv_hbm, w3_ref.at[pl.ds(7 * HS, HS)], w_sem.at[4]),
         pltpu.make_async_copy(wo_hbm, wo_ref, w_sem.at[5]),
         pltpu.make_async_copy(w_in_hbm.at[0], w_in_ref, w_sem.at[6]),
         pltpu.make_async_copy(w_back_hbm.at[0], w_back_ref, w_sem.at[7]),
@@ -637,7 +639,8 @@
 
     to_x, to_y = near_x * 2 + core, near_y * 2 + core
     mine = core * part
-    twin = send(0, me, 0, rows, partner)
+    twin = send(0, me, (1 - core) * part, part, partner)
+    rest = send(15, me, mine, part, partner)
     own, passed, relays, last = [], [], [], []
     for k in (0, 1):
         from_x, from_y, across = near_x * 2 + k, near_y * 2 + k, (3 - chip) * 2 + k
@@ -658,6 +661,7 @@
         )
         last.append(send(13 + k, across, mine, part, partner))
     twin.start()
+    rest.start()
 
     @pl.when(core == 0)
     def _():
@@ -665,9 +669,9 @@
             c.start()
 
     blank = jnp.zeros((HS, width), bf)
-    for i in (1, 3, 5, 6):
+    for i in (1, 3, 5):
         w3_ref[pl.ds(i * HS, HS), :] = blank
-    for c in loads[3:10]:
+    for c in loads[3:9]:
         c.wait()
 
     def row_copy(turn, block):
@@ -694,22 +698,47 @@
             r_out[turn - 1, block] = taken[turn * cap : (turn + 1) * cap]
             row_copy(turn, block).start()
 
-    def project(block, value):
-        at = pl.ds(pl.multiple_of(block * rows, rows), rows)
+    def project(spot, value):
+        at = pl.ds(pl.multiple_of(spot * rows, rows), rows)
         normed = rms_scale(value, gain_attn_ref[...]).astype(bf)
         three = lax.dot_general(normed, w3_ref[...], LAST, preferred_element_type=f32)
         q_all[at, :] = three[:, 0:wide].astype(bf)
         k_all[at, :] = three[:, wide : 2 * wide].astype(bf)
         lane = iota((rows, wide), 1)
-        v_all[0, at, :] = jnp.where(lane < HS, three[:, 2 * wide : 3 * wide], 1.0).astype(bf)
-        v_all[1, at, :] = jnp.where(lane < HS, 1.0, three[:, 3 * wide : 4 * wide]).astype(bf)
-
-    def take(block):
+        v_all[at, :] = jnp.where(lane < HS, three[:, 2 * wide : 3 * wide], 1.0).astype(bf)
+
+    def take(block, spot):
         value = x_all[block]
         route(block, value)
-        project(block, value)
-
-    take(me)
+        project(spot, value)
+
+    scale = score_gain / math.sqrt(HS) * math.log2(math.e)
+
+    def update(spot, spots, first, count, fresh):
+        at = pl.ds(spot * rows, spots * rows)
+        keys = pl.ds(first * rows, count * rows)
+        scores = lax.dot_general(q_all[at, :], k_all[keys, :], LAST, preferred_element_type=f32)
+        top = jnp.broadcast_to(
+            jnp.max(scores, axis=1, keepdims=True), (spots * rows, wide)
+        )
+        if not fresh:
+            known = top_ref[at, :]
+            top = jnp.maximum(top, known)
+        shift = jnp.concatenate([top * scale] * (count * rows // wide), axis=1)
+        weights = jnp.exp2(scores * scale - shift)
+        both = jnp.dot(weights.astype(bf), v_all[keys, :], preferred_element_type=f32)
+        if not fresh:
+            both = both + sum_ref[at, :] * jnp.exp2(known * scale - top * scale)
+        sum_ref[at, :] = both
+        top_ref[at, :] = top
+
+    def match(chip):
+        places = [place_all[2 * chip + side][0:1, :] for side in (0, 1)]
+        cells_ref[chip] = one_hot(
+            iota((owners * cap, 2 * rows), 0) == jnp.concatenate(places, axis=1)
+        )
+
+    take(me, core)
     twin.wait_recv()
 
     @pl.when(core == 1)
@@ -725,27 +754,6 @@
     wo_all[me] = wo_ref[...]
     places = bulk(place_all.at[pl.ds(0, n - 1)], p_send, p_recv)
     places.wait_recv()
-    take(partner)
-    for k in (0, 1):
-        for c, p, r in zip(own[k], passed[k], relays[k]):
-            c.wait_recv()
-            p.start()
-            r.start()
-        if k == 1:
-            o.begin()
-        for p, near in zip(passed[k], (near_x, near_y)):
-            p.wait_recv()
-            take(near * 2 + k)
-    for k in (0, 1):
-        for r in relays[k]:
-            r.wait_recv()
-        last[k].start()
-    for k in (0, 1):
-        last[k].wait_recv()
-        take((3 - chip) * 2 + k)
-
-    scale = score_gain / math.sqrt(HS) * math.log2(math.e)
-
     def mixed_copy(turn, d, j):
         to, c = plane(turn), lax.rem(me + d, n)
         lanes = pl.ds(pl.multiple_of(me * wide, wide), wide)
@@ -778,34 +786,61 @@
 
         each(turn, some)
 
-    def attend(first, last):
-        @pl.loop(first, last)
-        def _(j):
-            for side in (0, 1):
-                block = 2 * j + side
-                at = pl.ds(pl.multiple_of(block * rows, rows), rows)
-                scores = lax.dot_general(
-                    q_all[at, :], k_all[...], LAST, preferred_element_type=f32
-                )
-                top = jnp.max(scores, axis=1, keepdims=True)
-                weights = jnp.exp2(scores * scale - top * scale)
-                both = jnp.dot(weights.astype(bf), v_all[side], preferred_element_type=f32)
-                total = pltpu.roll(both, HS, 1)
-                mine = (iota((rows, wide), 1) // HS) == side
-                mix_ref[pl.ds(side * rows, rows), :] = jnp.where(mine, both / total, 0.0).astype(bf)
-            places = jnp.concatenate([place_all[2 * j][0:1, :], place_all[2 * j + 1][0:1, :]], axis=1)
-            spots = one_hot(iota((owners * cap, 2 * rows), 0) == places)
-            spread = jnp.dot(spots, mix_ref[...], preferred_element_type=f32).astype(bf)
-            m_out[:, j] = spread.reshape(owners, cap, wide)
-            each(2, lambda turn, d: mixed_copy(turn, d, j).start())
-            each(0, lambda turn, d: mixed_copy(turn, d, j).start())
-            mixed_own(j).start()
-
-    pl.semaphore_wait(ready, planes - 1)
-    attend(0, pairs - 1)
+    def finish(chip, spots):
+        for side, spot in enumerate(spots):
+            both = sum_ref[pl.ds(spot * rows, rows), :]
+            mixed = jnp.where(iota((rows, wide), 1) < HS, both / pltpu.roll(both, HS, 1), 0.0)
+            if side:
+                mixed = pltpu.roll(mixed, HS, 1)
+            mix_ref[pl.ds(side * rows, rows), :] = mixed.astype(bf)
+        spread = jnp.dot(cells_ref[chip], mix_ref[...], preferred_element_type=f32).astype(bf)
+        m_out[:, chip] = spread.reshape(owners, cap, wide)
+        each(2, lambda turn, d: mixed_copy(turn, d, chip).start())
+        each(0, lambda turn, d: mixed_copy(turn, d, chip).start())
+        mixed_own(chip).start()
+
+    rest.wait_recv()
+    take(partner, 1 - core)
+    update(0, 2, 0, 2, True)
+    for at in range(pairs):
+        match(at)
+    for c, p, r in zip(own[0], passed[0], relays[0]):
+        c.wait_recv()
+        p.start()
+        r.start()
+    for i, near in enumerate((near_x, near_y)):
+        passed[0][i].wait_recv()
+        take(near * 2, 2 + i)
+    update(0, 2, 2, 2, False)
+    update(2, 2, 0, 4, True)
+    for c, p, r in zip(own[1], passed[1], relays[1]):
+        c.wait_recv()
+        p.start()
+        r.start()
+    for i, near in enumerate((near_x, near_y)):
+        passed[1][i].wait_recv()
+        take(near * 2 + 1, 4 + i)
+    update(0, 4, 4, 2, False)
+    for r in relays[0]:
+        r.wait_recv()
+    last[0].start()
+    o.begin()
+    update(4, 2, 0, 6, True)
+    for r in relays[1]:
+        r.wait_recv()
+    last[1].start()
+    for k in (0, 1):
+        last[k].wait_recv()
+        take((3 - chip) * 2 + k, 6 + k)
+    update(0, 6, 6, 2, False)
     o.twin.wait_recv()
     o.relay()
-    attend(pairs - 1, pairs)
+    pl.semaphore_wait(ready, planes - 1)
+    finish(chip, (0, 1))
+    finish(near_x, (2, 4))
+    finish(near_y, (3, 5))
+    update(6, 2, 0, 8, True)
+    finish(3 - chip, (6, 7))
     o.diagonal()
 
     def seat(t):
@@ -828,7 +863,7 @@
     for z in range(planes):
         touched = touched + jnp.sum(picks_ref[z].astype(f32), axis=1, keepdims=True)
     acc_ref[...] = jnp.where(touched > 0.5, 0.0, doc_ref[...].astype(f32))
-    for c in loads[10:]:
+    for c in loads[9:]:
         c.wait()
     for _, c in o.passed:
         c.wait_recv()
@@ -892,7 +927,7 @@
         bulk(back_ref.at[0, pl.ds(0, count)], b_send.at[turn], b_recv.at[turn]).wait_send()
         if turn:
             bulk(r_in.at[0], r_send.at[turn], r_recv.at[turn]).wait_send()
-    for c in (twin, *last):
+    for c in (twin, rest, *last):
         c.wait_send()
     for c in own + passed + relays:
         c[0].wait_send()
@@ -940,7 +975,7 @@
             pltpu.VMEM((1, width), f32),
             pltpu.VMEM((1, width), f32),
             pltpu.VMEM((shard, width), bf),
-            pltpu.VMEM((8 * HS, width), bf),
+            pltpu.VMEM((6 * HS, width), bf),
             pltpu.VMEM(w_out.shape, bf),
             pltpu.VMEM(w_in.shape[1:], bf),
             pltpu.VMEM(w_back.shape[1:], bf),
@@ -948,8 +983,11 @@
             pltpu.VMEM((n, rows, width), bf),
             pltpu.VMEM((n * rows, wide), bf),
             pltpu.VMEM((n * rows, wide), bf),
-            pltpu.VMEM((2, n * rows, wide), bf),
+            pltpu.VMEM((n * rows, wide), bf),
+            pltpu.VMEM((n * rows, wide), f32),
+            pltpu.VMEM((n * rows, wide), f32),
             pltpu.VMEM((2 * rows, wide), bf),
+            pltpu.VMEM((n // 2, owners * cap, 2 * rows), bf),
             pltpu.VMEM((owners, pairs, cap, wide), bf),
             pltpu.VMEM((planes, pairs, cap, n * wide), bf),
             pltpu.VMEM((n,) + w_out.shape, bf),
@@ -965,8 +1003,8 @@
             sems((12,)),
             sems(()),
             sems(()),
-            sems((15,)),
-            sems((15,)),
+            sems((16,)),
+            sems((16,)),
             sems((copies,)),
             sems((copies,)),
             sems((planes,)),

time: 72.3 us -> 71 us (0.982)
  Pallas kernels: 71.2 us -> 69.8 us
    pallas_call x1, Pallas kernels: 71.2 us -> 69.8 us  [whole(): pl.pallas_call(functools.partial(whole_kernel, planes, n, cap), out_shape...]
where the time goes in v2:
time: 71 us; the launch traced here: 70.8 us
  Pallas kernels  69.8 us (98%)
  local copies, waits for them, and re-layouts  0.97 us (1%)
    pallas_call x1, Pallas kernels, whole(): pl.pallas_call(functools.partial(whole_kernel, planes, n, cap), out_shape...  69.8 us

profile of v2, /device:TPU:0, one launch (start us, length us, event | category | flops | bytes accessed | tf_op | source)
XLA Modules:
  0.0 70.8 jit_solution(12954826104598678611)
XLA Ops:
  0.0 69.8 %whole.1 = bf16[512,1024]{1,0:T(8,128)(2,1)S(1)} custom-call(s32[1,256]{1,0:T(1,128)} %kept_hbm.1, s32[1,256]{1,0:T(1,128)} %bitcast.15, f32[1,1024]{1,0:T(1,128)} %bitcast.13, f32[1,1024]{1,0:T(1,128)} %bitcast.14, bf16[512,1024]{1,0:T(8,128)(2,1)} %bitcast.9, bf16[64,1024]{1,0:T(8,128)(2,1)} %bitcast.10, bf16[64,1024]{1,0:T(8,128)(2,1)} %bitcast.11, ...), custom_call_target="tpu_custom_call" | custom-call | tf_op jit(solution)/shard_map/whole/pallas_call | solution.py:967
  69.8 1.0 %copy.13 = bf16[1,512,1024]{2,1,0:T(8,128)(2,1)} copy(bf16[1,512,1024]{2,1,0:T(8,128)(2,1)S(1)} %bitcast.8) | data formatting | bytes 2097152

commit v3 on v2

--- a/solution.py
+++ b/solution.py
@@ -550,8 +550,6 @@
         pltpu.make_async_copy(w_in_hbm.at[0], w_in_ref, w_sem.at[6]),
         pltpu.make_async_copy(w_back_hbm.at[0], w_back_ref, w_sem.at[7]),
     ]
-    for c in loads:
-        c.start()
 
     barrier = pltpu.get_barrier_semaphore()
 
@@ -567,6 +565,8 @@
             )
 
     column(barrier)
+    for c in loads:
+        c.start()
 
     def plane(g):
         high = lax.rem(dp // 2 + g // 2, 2)
@@ -631,7 +631,7 @@
         return pltpu.make_async_remote_copy(
             src_ref=ref,
             dst_ref=ref,
-            send_sem=x_send.at[ident],
+            send_sem=x_send,
             recv_sem=x_recv.at[ident],
             device_id={"ctx": target},
             device_id_type=MESH,
@@ -661,7 +661,6 @@
         )
         last.append(send(13 + k, across, mine, part, partner))
     twin.start()
-    rest.start()
 
     @pl.when(core == 0)
     def _():
@@ -738,7 +737,6 @@
             iota((owners * cap, 2 * rows), 0) == jnp.concatenate(places, axis=1)
         )
 
-    take(me, core)
     twin.wait_recv()
 
     @pl.when(core == 1)
@@ -746,8 +744,10 @@
         for c in own[0]:
             c.start()
 
+    rest.start()
     for c in own[1]:
         c.start()
+    take(me, core)
     for z in range(planes):
         cells = one_hot(iota((share, rows), 0) + z * share == place_own)
         picks_ref[z] = lax.dot_general(picks, cells, LAST, preferred_element_type=f32).astype(bf)
@@ -796,8 +796,7 @@
         spread = jnp.dot(cells_ref[chip], mix_ref[...], preferred_element_type=f32).astype(bf)
         m_out[:, chip] = spread.reshape(owners, cap, wide)
         each(2, lambda turn, d: mixed_copy(turn, d, chip).start())
-        each(0, lambda turn, d: mixed_copy(turn, d, chip).start())
-        mixed_own(chip).start()
+        each(3, lambda turn, d: mixed_copy(turn, d, chip).start())
 
     rest.wait_recv()
     take(partner, 1 - core)
@@ -857,8 +856,10 @@
             device_id_type=MESH,
         )
 
-    mixed_copies(3, lambda c: c.start())
+    mixed_copies(0, lambda c: c.start())
     mixed_copies(1, lambda c: c.start())
+    for j in range(pairs):
+        mixed_own(j).start()
     touched = jnp.zeros((shard, 1), f32)
     for z in range(planes):
         touched = touched + jnp.sum(picks_ref[z].astype(f32), axis=1, keepdims=True)
@@ -927,11 +928,7 @@
         bulk(back_ref.at[0, pl.ds(0, count)], b_send.at[turn], b_recv.at[turn]).wait_send()
         if turn:
             bulk(r_in.at[0], r_send.at[turn], r_recv.at[turn]).wait_send()
-    for c in (twin, rest, *last):
-        c.wait_send()
-    for c in own + passed + relays:
-        c[0].wait_send()
-        c[1].wait_send()
+    bulk(x_all.at[pl.ds(0, n - 1)], x_send, x_recv.at[0]).wait_send()
     o.drain()
 
 
@@ -1003,7 +1000,7 @@
             sems((12,)),
             sems(()),
             sems(()),
-            sems((16,)),
+            sems(()),
             sems((16,)),
             sems((copies,)),
             sems((copies,)),

time: 71 us -> 70.5 us (level)
  the two profiles are of different devices: /device:TPU:0 before, /device:TPU:9 now
where the time goes in v3:
time: 70.5 us; the launch traced here: 70.4 us
  Pallas kernels  69.4 us (98%)
  local copies, waits for them, and re-layouts  0.97 us (1%)
    pallas_call x1, Pallas kernels, whole(): pl.pallas_call(functools.partial(whole_kernel, planes, n, cap), out_shape...  69.4 us

profile of v3, /device:TPU:9, one launch (start us, length us, event | category | flops | bytes accessed | tf_op | source)
XLA Modules:
  0.0 70.4 jit_solution(16049844990131465695)
XLA Ops:
  0.0 69.4 %whole.1 = bf16[512,1024]{1,0:T(8,128)(2,1)S(1)} custom-call(s32[1,256]{1,0:T(1,128)} %kept_hbm.1, s32[1,256]{1,0:T(1,128)} %bitcast.15, f32[1,1024]{1,0:T(1,128)} %bitcast.13, f32[1,1024]{1,0:T(1,128)} %bitcast.14, bf16[512,1024]{1,0:T(8,128)(2,1)} %bitcast.9, bf16[64,1024]{1,0:T(8,128)(2,1)} %bitcast.10, bf16[64,1024]{1,0:T(8,128)(2,1)} %bitcast.11, ...), custom_call_target="tpu_custom_call" | custom-call | tf_op jit(solution)/shard_map/whole/pallas_call | solution.py:964
  69.4 1.0 %copy.13 = bf16[1,512,1024]{2,1,0:T(8,128)(2,1)} copy(bf16[1,512,1024]{2,1,0:T(8,128)(2,1)S(1)} %bitcast.8) | data formatting | bytes 2097152

commit v4 on v3

--- a/solution.py
+++ b/solution.py
@@ -842,8 +842,10 @@
     finish(3 - chip, (6, 7))
     o.diagonal()
 
+    inside = lax.rem((dp + 1) // 2, 2)
+
     def seat(t):
-        return lax.rem(t + planes // 2, planes)
+        return lax.rem(t + 2 * inside, planes)
 
     def back_copy(turn, d):
         to, c = plane(turn), lax.rem(me + d, n)

time: 70.5 us -> 70.2 us (level)
  the two profiles are of different devices: /device:TPU:9 before, /device:TPU:0 now
where the time goes in v4:
time: 70.2 us; the launch traced here: 70 us
  Pallas kernels  69.1 us (98%)
  local copies, waits for them, and re-layouts  0.97 us (1%)
    pallas_call x1, Pallas kernels, whole(): pl.pallas_call(functools.partial(whole_kernel, planes, n, cap), out_shape...  69.1 us

profile of v4, /device:TPU:0, one launch (start us, length us, event | category | flops | bytes accessed | tf_op | source)
XLA Modules:
  0.0 70.0 jit_solution(4149032306436332101)
XLA Ops:
  0.0 69.1 %whole.1 = bf16[512,1024]{1,0:T(8,128)(2,1)S(1)} custom-call(s32[1,256]{1,0:T(1,128)} %kept_hbm.1, s32[1,256]{1,0:T(1,128)} %bitcast.15, f32[1,1024]{1,0:T(1,128)} %bitcast.13, f32[1,1024]{1,0:T(1,128)} %bitcast.14, bf16[512,1024]{1,0:T(8,128)(2,1)} %bitcast.9, bf16[64,1024]{1,0:T(8,128)(2,1)} %bitcast.10, bf16[64,1024]{1,0:T(8,128)(2,1)} %bitcast.11, ...), custom_call_target="tpu_custom_call" | custom-call | tf_op jit(solution)/shard_map/whole/pallas_call | solution.py:966
  69.1 1.0 %copy.13 = bf16[1,512,1024]{2,1,0:T(8,128)(2,1)} copy(bf16[1,512,1024]{2,1,0:T(8,128)(2,1)S(1)} %bitcast.8) | data formatting | bytes 2097152

commit v5 on v4

--- a/solution.py
+++ b/solution.py
@@ -845,7 +845,7 @@
     inside = lax.rem((dp + 1) // 2, 2)
 
     def seat(t):
-        return lax.rem(t + 2 * inside, planes)
+        return (1 - inside) * t + inside * (2 - 2 * t + 5 * (t // 2))
 
     def back_copy(turn, d):
         to, c = plane(turn), lax.rem(me + d, n)

time: 70.2 us -> 68.8 us (0.980)
  the two profiles are of different devices: /device:TPU:0 before, /device:TPU:9 now
where the time goes in v5:
time: 68.8 us; the launch traced here: 68.6 us
  Pallas kernels  67.7 us (98%)
  local copies, waits for them, and re-layouts  0.97 us (1%)
    pallas_call x1, Pallas kernels, whole(): pl.pallas_call(functools.partial(whole_kernel, planes, n, cap), out_shape...  67.7 us

profile of v5, /device:TPU:9, one launch (start us, length us, event | category | flops | bytes accessed | tf_op | source)
XLA Modules:
  0.0 68.6 jit_solution(2377903949328338602)
XLA Ops:
  0.0 67.7 %whole.1 = bf16[512,1024]{1,0:T(8,128)(2,1)S(1)} custom-call(s32[1,256]{1,0:T(1,128)} %kept_hbm.1, s32[1,256]{1,0:T(1,128)} %bitcast.15, f32[1,1024]{1,0:T(1,128)} %bitcast.13, f32[1,1024]{1,0:T(1,128)} %bitcast.14, bf16[512,1024]{1,0:T(8,128)(2,1)} %bitcast.9, bf16[64,1024]{1,0:T(8,128)(2,1)} %bitcast.10, bf16[64,1024]{1,0:T(8,128)(2,1)} %bitcast.11, ...), custom_call_target="tpu_custom_call" | custom-call | tf_op jit(solution)/shard_map/whole/pallas_call | solution.py:966
  67.7 1.0 %copy.13 = bf16[1,512,1024]{2,1,0:T(8,128)(2,1)} copy(bf16[1,512,1024]{2,1,0:T(8,128)(2,1)S(1)} %bitcast.8) | data formatting | bytes 2097152
